TPU v7x, 32 devices: a whole 2x2x4 slice. The times are simulated.
32 devices in a mesh: seq: 8 (over y, x, core), tp: 4 (over z).
Axes of the slice: x: 2, y: 2, z: 4, core: 2. Of those that a mesh axis runs over, the one named last changes fastest.
Arguments:
- hidden: bfloat16 [4096, 4096], P('seq', 'tp'), may hold values from -6 to 6
- norm_gain: float32 [4096], P('tp'), may hold values from 0.5 to 1.5
- rank_down: bfloat16 [4096, 1024], P('tp'), may hold values from -0.09375 to 0.09375
- gate_up: bfloat16 [1024, 4096], P(None, 'tp'), may hold values from -0.1875 to 0.1875
- value_up: bfloat16 [1024, 4096], P(None, 'tp'), may hold values from -0.1875 to 0.1875
- state_up: bfloat16 [1024, 1024], P(None, 'tp'), may hold values from -0.1875 to 0.1875
- step_up: bfloat16 [1024, 64], P(None, 'tp'), may hold values from -0.1875 to 0.1875
- conv_value: float32 [4, 4096], P(None, 'tp'), may hold values from -3 to 3
- conv_state: float32 [4, 1024], P(None, 'tp'), may hold values from -3 to 3
- step_bias: float32 [64], P('tp'), may hold values from -6.9 to -2.3
- decay_log: float32 [64], P('tp'), may hold values from -11 to 2.77
- skip_gain: float32 [64], P('tp'), may hold values from 0.5 to 1.5
- gate_gain: float32 [4096], P('tp'), may hold values from 0.5 to 1.5
- out_down: bfloat16 [4096, 1024], P('tp'), may hold values from -0.09375 to 0.09375
- out_up: bfloat16 [1024, 4096], P(None, 'tp'), may hold values from -0.1875 to 0.1875
Outputs:
- block_out: bfloat16 [4096, 4096], P('seq', 'tp')
All inputs are finite; a program needn't handle non-finite values.
Results may differ from a plain program's by a relative error of at most 0.012.
Values may be sent and summed in bfloat16 or wider, within the bound.
A program may use at most 64 MiB of HBM per device.

v0:
```python
import jax
import jax.numpy as jnp
from jax import lax
from jax.sharding import PartitionSpec as P

HEAD_DIM = 64
NSTATE = 128
GROUPS = 4
epsilon = 1e-05
highest = lax.Precision.HIGHEST


def shifted(shard, axis, by):
    peers = lax.axis_size(axis)
    pairs = [(i, i + by) for i in range(peers) if 0 <= i + by < peers]
    return lax.ppermute(shard, axis, pairs)


def entering(part, axis, combine, identity):
    place = lax.axis_index(axis)
    gathered = jax.tree.map(lambda a: lax.all_gather(a, axis), part)
    state = jax.tree.map(lambda a, e: jnp.zeros_like(a) + jnp.asarray(e, a.dtype), part, identity)

    def one(lap, state):
        return combine(
            state, jax.tree.map(lambda a: lax.dynamic_index_in_dim(a, lap, 0, False), gathered)
        )

    return lax.fori_loop(0, place, one, state)


def contract_rows(left, right):
    return lax.dot_general(
        left, right, (((0,), (0,)), ((), ())), preferred_element_type=jnp.float32
    )


def contract_columns(columns, rows):
    return lax.dot_general(
        columns, rows, (((0,), (1,)), ((), ())), preferred_element_type=jnp.float32
    )


def depthwise(rim_rows, current, weights):
    joined = jnp.concatenate([rim_rows, current], axis=0).astype(jnp.float32)
    length = current.shape[0]
    result = jnp.zeros(current.shape, jnp.float32)
    for offset in range(weights.shape[0]):
        result = result + weights[offset] * joined[offset : offset + length]
    return jax.nn.silu(result).astype(jnp.bfloat16)


def on_device(
    hidden,
    norm_gain,
    rank_down,
    gate_up,
    value_up,
    state_up,
    step_up,
    conv_value,
    conv_state,
    step_bias,
    decay_log,
    skip_gain,
    gate_gain,
    out_down,
    out_up,
):
    tokens = hidden.shape[0]
    tp_count = lax.axis_size("tp")
    tp_index = lax.axis_index("tp")
    model_width = hidden.shape[1] * tp_count
    hidden_wide = hidden.astype(jnp.float32)
    local_squares = jnp.sum(hidden_wide * hidden_wide, axis=1)
    scaled = (hidden_wide * norm_gain).astype(jnp.bfloat16)
    up_weights = (gate_up, value_up, state_up, step_up)
    partial_value = jnp.dot(scaled, rank_down, preferred_element_type=jnp.float32)
    summed, total_squares = lax.psum((partial_value, local_squares), "tp")
    factor = lax.rsqrt(total_squares / model_width + epsilon)
    reduced = (summed * factor[:, None]).astype(jnp.bfloat16)
    projected = tuple(
        (jnp.dot(reduced, weight, preferred_element_type=jnp.float32) for weight in up_weights)
    )
    gate_pre = projected[0].astype(jnp.bfloat16)
    value_pre = projected[1].astype(jnp.bfloat16)
    state_pre = projected[2].astype(jnp.bfloat16)
    step_pre = projected[3].astype(jnp.bfloat16)
    rim_start = tokens - conv_value.shape[0] + 1
    rim_value, rim_state = shifted((value_pre[rim_start:], state_pre[rim_start:]), "seq", 1)
    value_act = depthwise(rim_value, value_pre, conv_value)
    state_act = depthwise(rim_state, state_pre, conv_state)
    state_all = lax.all_gather(state_act, "tp", axis=1, tiled=True)
    heads_local = decay_log.shape[0]
    heads_total = heads_local * tp_count
    group_index = tp_index * heads_local // (heads_total // GROUPS)
    inward = lax.dynamic_slice_in_dim(state_all, group_index * NSTATE, NSTATE, 1).astype(
        jnp.float32
    )
    outward = lax.dynamic_slice_in_dim(
        state_all, (GROUPS + group_index) * NSTATE, NSTATE, 1
    ).astype(jnp.float32)
    step_size = jax.nn.softplus(step_pre.astype(jnp.float32) + step_bias)
    log_decay = jnp.cumsum(-jnp.exp(decay_log) * step_size, axis=0)
    values = value_act.astype(jnp.float32).reshape(tokens, heads_local, HEAD_DIM)
    coupling = jnp.dot(outward, inward.T, precision=highest)
    positions = jnp.arange(tokens)
    causal = positions[:, None] >= positions[None, :]
    spread = log_decay.T[:, :, None] - log_decay.T[:, None, :]
    attenuation = jnp.where(causal[None], jnp.exp(jnp.where(causal[None], spread, 0.0)), 0.0)
    mixing = coupling[None] * attenuation * step_size.T[:, None, :]
    within = jnp.einsum("hts,shp->thp", mixing, values, precision=highest)
    ending = jnp.exp(log_decay[-1][None, :] - log_decay) * step_size
    local_state = jnp.einsum("sh,shp,sn->hpn", ending, values, inward, precision=highest)
    local_decay = jnp.exp(log_decay[-1])

    def combine(earlier, later):
        return (earlier[0] * later[0], later[0][:, None, None] * earlier[1] + later[1])

    prefix = entering(
        (local_decay, local_state),
        "seq",
        combine,
        (jnp.ones_like(local_decay), jnp.zeros_like(local_state)),
    )
    incoming = prefix[1]
    carried_in = jnp.exp(log_decay)[:, :, None] * jnp.einsum(
        "tn,hpn->thp", outward, incoming, precision=highest
    )
    mixed = (within + carried_in + skip_gain[None, :, None] * values).reshape(
        tokens, heads_local * HEAD_DIM
    )
    gated = mixed * jax.nn.silu(gate_pre.astype(jnp.float32))
    group_width = heads_total * HEAD_DIM // GROUPS
    selector = (jnp.arange(GROUPS) == group_index).astype(jnp.float32)
    group_sums = lax.psum(jnp.sum(gated * gated, axis=1)[:, None] * selector[None, :], "tp")
    own_sum = jnp.sum(group_sums * selector[None, :], axis=1)
    normed = (gated * lax.rsqrt(own_sum / group_width + epsilon)[:, None] * gate_gain).astype(
        jnp.bfloat16
    )
    out_share = lax.psum_scatter(
        contract_columns(out_down, normed), "tp", scatter_dimension=0, tiled=True
    ).astype(jnp.bfloat16)
    update = contract_rows(lax.all_gather(out_share, "tp", axis=0, tiled=True), out_up)
    return (hidden_wide + update).astype(jnp.bfloat16)


def solution(mesh):
    return jax.shard_map(
        on_device,
        mesh=mesh,
        in_specs=(
            P("seq", "tp"),
            P("tp"),
            P("tp", None),
            P(None, "tp"),
            P(None, "tp"),
            P(None, "tp"),
            P(None, "tp"),
            P(None, "tp"),
            P(None, "tp"),
            P("tp"),
            P("tp"),
            P("tp"),
            P("tp"),
            P("tp", None),
            P(None, "tp"),
        ),
        out_specs=P("seq", "tp"),
        check_vma=False,
    )
```

profile of v0, /device:TPU:0, one launch (start us, length us, event | category | flops | bytes accessed | tf_op | source)
XLA Modules:
  0.0 310.0 jit_solution(9953234598632457863)
XLA Ops:
  6.5 4.6 %fusion.29 = f32[512,1024]{1,0:T(8,128)} fusion(bf16[1024,1024]{1,0:T(8,128)(2,1)} %param.19, bf16[512,1024]{1,0:T(8,128)(2,1)} %param.17, f32[1024]{0:T(1024)} %param.18), kind=kOutput, calls=%fused_computation.51 | convolution fusion | flops 1075314688 | bytes 5246976 | tf_op jit(solution)/shard_map/dot_general | solution.py:78
  12.7 13.9 %psum.22 = f32[512]{0:T(512)S(1)} all-reduce(f32[512]{0:T(512)S(1)} %fusion.20), channel_id=1, replica_groups=mesh['seq'=8,'tp'=4] {'tp'}, use_global_device_ids=true, to_apply=%region_2.0 | all-reduce | flops 512 | bytes 4096 | tf_op jit(solution)/shard_map/psum | solution.py:79
  27.2 73.1 %all-reduce.2.cloned.1.call-done = f32[512,1024]{1,0:T(8,128)} async-done(((f32[512,1024]{1,0:T(8,128)}), f32[512,1024]{1,0:T(8,128)}) %all-reduce.2.cloned.1.call-update) | async-done | bytes 2097168 | tf_op jit(solution)/shard_map/psum | solution.py:79
  100.3 1.8 multiply_convert_fusion.2
  103.7 2.0 collective-permute-start.1
  107.7 1.7 multiply_convert_fusion.4
  109.5 2.8 convolution_convert_fusion.1
  112.4 3.4 %collective-permute-start = (bf16[3,1024]{1,0:T(4,128)(2,1)S(1)}, bf16[3,1024]{1,0:T(4,128)(2,1)S(1)}, u32[]{:S(2)}, u32[]{:S(2)}) collective-permute-start(bf16[3,1024]{1,0:T(4,128)(2,1)S(1)} %slice.85), channel_id=1, source_target_pairs={{0,4},{4,8},{8,12},{12,16},{16,20},{20,24},{24,28},{1,5},{5,9},{9,... | collective-permute-start | bytes 18440 | tf_op jit(solution)/shard_map/ppermute | solution.py:16
  118.2 1.3 copy.29
  119.6 21.0 %all-gather.6.cloned.1.call-done = bf16[512,1024]{1,0:T(8,128)(2,1)} async-done(((bf16[512,256]{1,0:T(8,128)(2,1)}), bf16[512,1024]{1,0:T(8,128)(2,1)}) %all-gather.6.cloned.1.call-update) | async-done | bytes 1048592 | tf_op jit(solution)/shard_map/all_gather | solution.py:93
  140.6 3.2 %fusion.13 = f32[16,64,128]{2,1,0:T(8,128)} fusion(bf16[512,16,64]{0,2,1:T(8,128)(2,1)} %bitcast.86, f32[512,16]{0,1:T(8,128)S(1)} %get-tuple-element.63, bf16[512,1024]{1,0:T(8,128)(2,1)} %all-gather.6.cloned.1.call-done, s32[]{:T(128)S(6)} %select_n.35), kind=kOutput, calls=%fused_computation.22 | convolution fusion | flops 806354944 | bytes 1736708 | tf_op jit(solution)/shard_map/sh,shp,sn->hpn/dot_general | solution.py:114
  143.9 7.9 %all-gather.1 = f32[8,1,16]{2,1,0:T(1,128)S(1)} all-gather(f32[1,1,16]{2,1,0:T(1,128)S(1)} %bitcast.100), channel_id=1, replica_groups=mesh['seq'=8,'tp'=4] {'seq'}, dimensions={0}, use_global_device_ids=true | all-gather | bytes 576 | tf_op jit(solution)/shard_map/all_gather | solution.py:21
  151.9 2.3 fusion.42
  154.1 24.7 %all-gather.10.cloned.1.call-done = f32[128,64,128]{2,1,0:T(8,128)} async-done(((f32[16,64,128]{2,1,0:T(8,128)}), f32[128,64,128]{2,1,0:T(8,128)}) %all-gather.10.cloned.1.call-update) | async-done | bytes 4194320 | tf_op jit(solution)/shard_map/all_gather | solution.py:21
  179.1 2.0 fusion.39
  181.2 14.3 %fusion.14 = f32[512,16,64]{0,2,1:T(8,128)} fusion(bf16[512,16,64]{0,2,1:T(8,128)(2,1)S(1)} %bitcast.87, f32[512,16,64]{0,2,1:T(8,128)S(1)} %fusion.39, f32[16,512]{1,0:T(8,128)S(1)} %get-tuple-element.66, f32[16,512]{1,0:T(8,128)S(1)} %get-tuple-element.64, f32[512,512]{1,0:T(8,128)S(1)} %copy-done.6, pred[512,512]{1,0:T(8,128)(4,1)S(1)} %iota_compare_fusion, ...), kind=kOutput, calls=%fused_computation.23 | convolution fusion | flops 3244818432 | bytes 6651968 | tf_op jit(solution)/shard_map/hts,shp->thp/dot_general | solution.py:112
  195.5 3.0 copy.32
  198.5 4.5 %multiply_reduce_fusion = (f32[512]{0:T(512)S(1)}, f32[512,1024]{1,0:T(8,128)}) fusion(f32[512,1024]{1,0:T(8,128)} %copy.32, bf16[512,1024]{1,0:T(8,128)(2,1)S(1)} %copy-done.3, bf16[1024,1024]{1,0:T(8,128)(2,1)S(1)} %copy-done), kind=kOutput, calls=%fused_computation.40 | convolution fusion | flops 1078459904 | bytes 7342080 | tf_op jit(solution)/shard_map/dot_general | solution.py:83
  203.1 11.8 %psum.23 = f32[512,4]{0,1:T(4,128)S(1)} all-reduce(f32[512,4]{0,1:T(4,128)S(1)} %broadcast_multiply_fusion), channel_id=1, replica_groups=mesh['seq'=8,'tp'=4] {'tp'}, use_global_device_ids=true, to_apply=%region_8.9 | all-reduce | flops 2048 | bytes 16384 | tf_op jit(solution)/shard_map/psum | solution.py:136
  215.0 4.8 %convolution_bitcast_fusion = f32[1024,512]{0,1:T(8,128)} fusion(bf16[1024,1024]{1,0:T(8,128)(2,1)} %param.30, f32[512,1024]{1,0:T(8,128)} %get-tuple-element.77, f32[1024]{0:T(1024)S(1)} %copy-done.12, f32[512]{0:T(512)S(1)} %add_rsqrt_fusion), kind=kOutput, calls=%fused_computation.43 | convolution fusion | flops 1075314688 | bytes 6297600 | tf_op jit(solution)/shard_map/dot_general | solution.py:39
  219.9 48.4 %reduce-scatter.2.cloned.1.call-done = f32[256,512]{0,1:T(8,128)} async-done(((f32[1024,512]{0,1:T(8,128)}), f32[256,512]{0,1:T(8,128)}) %reduce-scatter.2.cloned.1.call-update) | async-done | bytes 524304 | tf_op jit(solution)/shard_map/reduce_scatter | solution.py:141
  268.3 1.8 convert_element_type.79
  270.1 29.3 %all-gather.8.cloned.1.call-done = bf16[1024,512]{0,1:T(8,128)(2,1)} async-done(((bf16[256,512]{0,1:T(8,128)(2,1)}), bf16[1024,512]{0,1:T(8,128)(2,1)}) %all-gather.8.cloned.1.call-update) | async-done | bytes 1048592 | tf_op jit(solution)/shard_map/all_gather | solution.py:144
  299.4 4.1 %fusion.21 = bf16[512,1024]{1,0:T(8,128)(2,1)} fusion(bf16[512,1024]{1,0:T(8,128)(2,1)S(1)} %copy-done.5, bf16[1024,512]{0,1:T(8,128)(2,1)} %all-gather.8.cloned.1.call-done, bf16[1024,1024]{1,0:T(8,128)(2,1)} %param.31), kind=kOutput, calls=%fused_computation.30 | convolution fusion | flops 1075314688 | bytes 5242880 | tf_op jit(solution)/shard_map/dot_general | solution.py:33
  (70 shorter events, 8.8 us)
Async XLA Ops:
  6.5 192.0 %copy-start = (bf16[1024,1024]{1,0:T(8,128)(2,1)S(1)}, bf16[1024,1024]{1,0:T(8,128)(2,1)}, u32[]{:S(2)}) copy-start(bf16[1024,1024]{1,0:T(8,128)(2,1)} %param.20) | copy-start | bytes 6291460
  6.5 93.8 %all-reduce.2.cloned.1.call-start = ((), (), s32[]{:S(2)}) async-start(), calls=%async_computation.1 | async-start | bytes 4194304 | tf_op jit(solution)/shard_map/psum | solution.py:79
  11.2 1.2 copy-start.4
  11.2 15.4 %copy-start.13 = (f32[16]{0:T(128)S(1)}, f32[16]{0:T(128)}, u32[]{:S(2)}) copy-start(f32[16]{0:T(128)} %param.27) | copy-start | bytes 196
  11.2 15.4 %copy-start.9 = (f32[4,256]{1,0:T(4,128)S(1)}, f32[4,256]{1,0:T(4,128)}, u32[]{:S(2)}) copy-start(f32[4,256]{1,0:T(4,128)} %param.25) | copy-start | bytes 12292
  11.2 16.0 %copy-start.8 = (f32[4,1024]{1,0:T(4,128)S(1)}, f32[4,1024]{1,0:T(4,128)}, u32[]{:S(2)}) copy-start(f32[4,1024]{1,0:T(4,128)} %param.24) | copy-start | bytes 49156
  11.2 129.4 %all-gather.6.cloned.1.call-start = ((), (), s32[]{:S(2)}) async-start(), calls=%async_computation.2 | async-start | bytes 1310720 | tf_op jit(solution)/shard_map/all_gather | solution.py:93
  12.4 89.8 %copy-start.7 = (bf16[1024,16]{0,1:T(8,128)(2,1)S(1)}, bf16[1024,16]{0,1:T(8,128)(2,1)}, u32[]{:S(2)}) copy-start(bf16[1024,16]{0,1:T(8,128)(2,1)} %param.23) | copy-start | bytes 98308
  12.4 89.8 %copy-start.10 = (f32[16]{0:T(128)S(1)}, f32[16]{0:T(128)}, u32[]{:S(2)}) copy-start(f32[16]{0:T(128)} %param.26) | copy-start | bytes 196
  100.3 2.3 copy-start.11
  102.2 7.3 %copy-start.2 = (bf16[512,1024]{1,0:T(8,128)(2,1)}, bf16[512,1024]{1,0:T(8,128)(2,1)S(1)}, u32[]{:S(2)}) copy-start(bf16[512,1024]{1,0:T(8,128)(2,1)S(1)} %multiply_convert_fusion.2) | copy-start | bytes 3145732
  103.7 3.3 %collective-permute-start.1 = (bf16[3,256]{1,0:T(4,128)(2,1)}, bf16[3,256]{1,0:T(4,128)(2,1)}, u32[]{:S(2)}, u32[]{:S(2)}) collective-permute-start(bf16[3,256]{1,0:T(4,128)(2,1)} %slice.90), channel_id=1, source_target_pairs={{0,4},{4,8},{8,12},{12,16},{16,20},{20,24},{24,28},{1,5},{5,9},{9,... | collective-permute-start | bytes 4616 | tf_op jit(solution)/shard_map/ppermute | solution.py:16
  109.5 69.4 %all-gather.10.cloned.1.call-start = ((), (), s32[]{:S(2)}) async-start(), calls=%async_computation.5 | async-start | bytes 4718592 | tf_op jit(solution)/shard_map/all_gather | solution.py:21
  112.4 4.3 %collective-permute-start = (bf16[3,1024]{1,0:T(4,128)(2,1)S(1)}, bf16[3,1024]{1,0:T(4,128)(2,1)S(1)}, u32[]{:S(2)}, u32[]{:S(2)}) collective-permute-start(bf16[3,1024]{1,0:T(4,128)(2,1)S(1)} %slice.85), channel_id=1, source_target_pairs={{0,4},{4,8},{8,12},{12,16},{16,20},{20,24},{24,28},{1,5},{5,9},{9,... | collective-permute-start | bytes 18440 | tf_op jit(solution)/shard_map/ppermute | solution.py:16
  143.8 124.5 %reduce-scatter.2.cloned.1.call-start = ((), (), s32[]{:S(2)}) async-start(), calls=%async_computation.3 | async-start | bytes 2621440 | tf_op jit(solution)/shard_map/reduce_scatter | solution.py:141
  179.1 2.1 copy-start.1
  179.1 2.1 copy-start.6
  179.1 2.1 copy-start.14
  195.5 3.0 copy-start.3
  198.5 16.5 %copy-start.12 = (f32[1024]{0:T(1024)S(1)}, f32[1024]{0:T(1024)}, u32[]{:S(2)}) copy-start(f32[1024]{0:T(1024)} %param.29) | copy-start | bytes 12292
  219.8 79.5 %copy-start.5 = (bf16[512,1024]{1,0:T(8,128)(2,1)S(1)}, bf16[512,1024]{1,0:T(8,128)(2,1)}, u32[]{:S(2)}) copy-start(bf16[512,1024]{1,0:T(8,128)(2,1)} %param.17) | copy-start | bytes 3145732
  219.9 79.5 %all-gather.8.cloned.1.call-start = ((), (), s32[]{:S(2)}) async-start(), calls=%async_computation.4 | async-start | bytes 1310720 | tf_op jit(solution)/shard_map/all_gather | solution.py:144
Sparse Core Ops, SparseCore 0:
  11.3 88.9 all-reduce.1
  109.6 30.9 all-gather.5
  143.9 34.8 all-gather.9
  220.0 48.2 reduce-scatter.1
  270.2 29.1 all-gather.7
where the time goes:
time: 311 us; the launch traced here: 310 us
  waiting for transfers between devices  197 us (63%)
  matrix products  43.6 us (14%)
  blocking collectives  33.6 us (11%)
  between operations  13.4 us (4%)
  other arithmetic  9.56 us (3%)
  local copies, waits for them, and re-layouts  7.12 us (2%)
  starting transfers between devices  5.58 us (2%)
    psum x1, waiting for transfers between devices, on_device(): summed, total_squares = lax.psum((partial_value, local_squares), 'tp')  73.1 us
    reduce_scatter x1, waiting for transfers between devices, on_device(): lax.psum_scatter(contract_columns(out_down, normed), 'tp', scatter_dimens...  48.4 us
    all_gather x1, waiting for transfers between devices, on_device(): lax.all_gather(out_share, 'tp', axis=0, tiled=True)  29.3 us
    all_gather x1, waiting for transfers between devices, entering(): gathered = jax.tree.map(lambda a: lax.all_gather(a, axis), part)  24.7 us
    all_gather x1, waiting for transfers between devices, on_device(): state_all = lax.all_gather(state_act, 'tp', axis=1, tiled=True)  21 us
    dot_general x1, matrix products, on_device(): within = jnp.einsum('hts,shp->thp', mixing, values, precision=highest)  14.3 us
    psum x1, blocking collectives, on_device(): summed, total_squares = lax.psum((partial_value, local_squares), 'tp')  13.9 us
    psum x1, blocking collectives, on_device(): lax.psum(jnp.sum(gated * gated, axis=1)[:, None] * selector[None, :], 'tp')  11.8 us
  transfers between devices with their start and end apart: 7, of which 6 were waited for; matrix products, arithmetic and copies ran while one was open for 3% of the time, Pallas kernels for 0%

commit v1 on v0

--- a/solution.py
+++ b/solution.py
@@ -90,7 +90,12 @@
     rim_value, rim_state = shifted((value_pre[rim_start:], state_pre[rim_start:]), "seq", 1)
     value_act = depthwise(rim_value, value_pre, conv_value)
     state_act = depthwise(rim_state, state_pre, conv_state)
-    state_all = lax.all_gather(state_act, "tp", axis=1, tiled=True)
+    ring = [state_act]
+    for hop in range(3):
+        ring.append(lax.ppermute(ring[-1], "tp", [(dev, (dev + 1) % 4) for dev in range(4)]))
+    state_all = jnp.roll(
+        jnp.concatenate(ring[::-1], axis=1), (lax.axis_index("tp") + 1) * ring[0].shape[1], axis=1
+    )
     heads_local = decay_log.shape[0]
     heads_total = heads_local * tp_count
     group_index = tp_index * heads_local // (heads_total // GROUPS)

time: 311 us -> 300 us (0.965)
  waiting for transfers between devices: 197 us -> 180 us
  local copies, waits for them, and re-layouts: 7.12 us -> 11.3 us
    ppermute x0 -> x3, waiting for transfers between devices: none -> 21.3 us  [on_device(): lax.ppermute(ring[-1], 'tp', [(dev, (dev + 1) % 4) for dev in range(4)])]
    all_gather x1 -> x0, waiting for transfers between devices: 21 us -> none  [on_device(): state_all = lax.all_gather(state_act, 'tp', axis=1, tiled=True)]
    all_gather x1, waiting for transfers between devices: 24.7 us -> 9.19 us  [entering(): gathered = jax.tree.map(lambda a: lax.all_gather(a, axis), part)]
  transfers between devices with their start and end apart: 7 -> 9, of which waited for: 6 -> 7; matrix products, arithmetic and copies ran while one was open for 3% -> 9% of each run, Pallas kernels for 0% -> 0%
where the time goes in v1:
time: 300 us
  waiting for transfers between devices  180 us (60%)
  matrix products  42.6 us (14%)
  blocking collectives  34.8 us (12%)
  between operations  13.6 us (5%)
  local copies, waits for them, and re-layouts  11.3 us (4%)
  other arithmetic  11.3 us (4%)
  starting transfers between devices  5.99 us (2%)
    psum x1, waiting for transfers between devices, on_device(): summed, total_squares = lax.psum((partial_value, local_squares), 'tp')  72.4 us
    reduce_scatter x1, waiting for transfers between devices, on_device(): lax.psum_scatter(contract_columns(out_down, normed), 'tp', scatter_dimens...  47.7 us
    all_gather x1, waiting for transfers between devices, on_device(): lax.all_gather(out_share, 'tp', axis=0, tiled=True)  29.3 us
    ppermute x3, waiting for transfers between devices, on_device(): lax.ppermute(ring[-1], 'tp', [(dev, (dev + 1) % 4) for dev in range(4)])  21.3 us
    dot_general x1, matrix products, on_device(): within = jnp.einsum('hts,shp->thp', mixing, values, precision=highest)  14.3 us
    psum x1, blocking collectives, on_device(): summed, total_squares = lax.psum((partial_value, local_squares), 'tp')  14 us
    psum x1, blocking collectives, on_device(): lax.psum(jnp.sum(gated * gated, axis=1)[:, None] * selector[None, :], 'tp')  11.9 us
    all_gather x1, waiting for transfers between devices, entering(): gathered = jax.tree.map(lambda a: lax.all_gather(a, axis), part)  9.19 us
  transfers between devices with their start and end apart: 9, of which 7 were waited for; matrix products, arithmetic and copies ran while one was open for 9% of the time, Pallas kernels for 0%

profile of v1, /device:TPU:0, one launch (start us, length us, event | category | flops | bytes accessed | tf_op | source)
XLA Modules:
  0.0 299.5 jit_solution(7248163469461940934)
XLA Ops:
  6.5 4.6 %fusion.27 = f32[512,1024]{1,0:T(8,128)} fusion(bf16[1024,1024]{1,0:T(8,128)(2,1)} %param.19, bf16[512,1024]{1,0:T(8,128)(2,1)} %param.17, f32[1024]{0:T(1024)} %param.18), kind=kOutput, calls=%fused_computation.51 | convolution fusion | flops 1075314688 | bytes 5246976 | tf_op jit(solution)/shard_map/dot_general | solution.py:78
  12.7 14.0 %psum.22 = f32[512]{0:T(512)S(1)} all-reduce(f32[512]{0:T(512)S(1)} %fusion.20), channel_id=1, replica_groups=mesh['seq'=8,'tp'=4] {'tp'}, use_global_device_ids=true, to_apply=%region_2.0 | all-reduce | flops 512 | bytes 4096 | tf_op jit(solution)/shard_map/psum | solution.py:79
  28.0 72.4 %all-reduce.2.cloned.1.call-done = f32[512,1024]{1,0:T(8,128)} async-done(((f32[512,1024]{1,0:T(8,128)}), f32[512,1024]{1,0:T(8,128)}) %all-reduce.2.cloned.1.call-update) | async-done | bytes 2097168 | tf_op jit(solution)/shard_map/psum | solution.py:79
  100.3 1.8 multiply_convert_fusion.2
  103.2 2.0 collective-permute-start.1
  108.3 3.4 %collective-permute-start = (bf16[3,1024]{1,0:T(4,128)(2,1)S(1)}, bf16[3,1024]{1,0:T(4,128)(2,1)S(1)}, u32[]{:S(2)}, u32[]{:S(2)}) collective-permute-start(bf16[3,1024]{1,0:T(4,128)(2,1)S(1)} %slice.85), channel_id=1, source_target_pairs={{0,4},{4,8},{8,12},{12,16},{16,20},{20,24},{24,28},{1,5},{5,9},{9,... | collective-permute-start | bytes 18440 | tf_op jit(solution)/shard_map/ppermute | solution.py:16
  114.9 8.8 %collective-permute-done.2 = bf16[512,256]{1,0:T(8,128)(2,1)S(1)} collective-permute-done((bf16[512,256]{1,0:T(8,128)(2,1)S(1)}, bf16[512,256]{1,0:T(8,128)(2,1)S(1)}, u32[]{:S(2)}, u32[]{:S(2)}) %collective-permute-start.2) | collective-permute-done | bytes 262176 | tf_op jit(solution)/shard_map/ppermute | solution.py:95
  124.1 8.7 %collective-permute-done.3 = bf16[512,256]{1,0:T(8,128)(2,1)S(1)} collective-permute-done((bf16[512,256]{1,0:T(8,128)(2,1)S(1)}, bf16[512,256]{1,0:T(8,128)(2,1)S(1)}, u32[]{:S(2)}, u32[]{:S(2)}) %collective-permute-start.3) | collective-permute-done | bytes 262176 | tf_op jit(solution)/shard_map/ppermute | solution.py:95
  132.9 2.2 multiply_convert_fusion.1
  135.2 2.3 copy.29
  137.4 3.7 %collective-permute-done.4 = bf16[512,256]{1,0:T(8,128)(2,1)S(1)} collective-permute-done((bf16[512,256]{1,0:T(8,128)(2,1)S(1)}, bf16[512,256]{1,0:T(8,128)(2,1)S(1)}, u32[]{:S(2)}, u32[]{:S(2)}) %collective-permute-start.4) | collective-permute-done | bytes 262176 | tf_op jit(solution)/shard_map/ppermute | solution.py:95
  144.2 2.0 fusion.13
  146.4 8.9 %all-gather.1 = f32[8,1,16]{2,1,0:T(1,128)S(1)} all-gather(f32[1,1,16]{2,1,0:T(1,128)S(1)} %bitcast.109), channel_id=1, replica_groups=mesh['seq'=8,'tp'=4] {'seq'}, dimensions={0}, use_global_device_ids=true | all-gather | bytes 576 | tf_op jit(solution)/shard_map/all_gather | solution.py:21
  156.8 14.3 %fusion = f32[16,64,512]{2,1,0:T(8,128)} fusion(bf16[512,16,64]{0,2,1:T(8,128)(2,1)S(1)} %bitcast.88, f32[16,512]{1,0:T(8,128)S(1)} %get-tuple-element.67, f32[16,512]{1,0:T(8,128)S(1)} %get-tuple-element.65, f32[512,512]{1,0:T(8,128)S(1)} %fusion.39, pred[512,512]{1,0:T(8,128)(4,1)S(1)} %iota_compare_fusion), kind=kOutput, calls=%fused_computation.2 | convolution fusion | flops 3242196992 | bytes 4521984 | tf_op jit(solution)/shard_map/hts,shp->thp/dot_general | solution.py:117
  171.1 9.2 %all-gather.7.cloned.1.call-done = f32[128,64,128]{2,1,0:T(8,128)} async-done(((f32[16,64,128]{2,1,0:T(8,128)}), f32[128,64,128]{2,1,0:T(8,128)}) %all-gather.7.cloned.1.call-update) | async-done | bytes 4194320 | tf_op jit(solution)/shard_map/all_gather | solution.py:21
  181.0 4.6 %fusion.14 = f32[512,16,64]{0,2,1:T(8,128)} fusion(bf16[512,16,64]{0,2,1:T(8,128)(2,1)} %bitcast.86, f32[16,64,512]{2,1,0:T(8,128)} %fusion, f32[16,64,128]{2,1,0:T(8,128)S(1)} %get-tuple-element.49, f32[16]{0:T(128)S(1)} %copy-done.21, f32[512,16]{0,1:T(8,128)S(1)} %get-tuple-element.62, bf16[512,2048]{1,0:T(8,128)(2,1)} %copy-done.9, s32[]{:T(128)S(6)} %dynamic_slice.24), kind=kOutput, calls=%fused_computation.23 | convolution fusion | flops 807927808 | bytes 5931076 | tf_op jit(solution)/shard_map/tn,hpn->thp/dot_general | solution.py:132
  185.6 3.0 copy.32
  188.6 4.5 %multiply_reduce_fusion = (f32[512]{0:T(512)S(1)}, f32[512,1024]{1,0:T(8,128)}) fusion(f32[512,1024]{1,0:T(8,128)} %copy.32, bf16[512,1024]{1,0:T(8,128)(2,1)S(1)} %copy-done.4, bf16[1024,1024]{1,0:T(8,128)(2,1)S(1)} %copy-done), kind=kOutput, calls=%fused_computation.40 | convolution fusion | flops 1078459904 | bytes 7342080 | tf_op jit(solution)/shard_map/dot_general | solution.py:83
  193.2 11.9 %psum.23 = f32[512,4]{0,1:T(4,128)S(1)} all-reduce(f32[512,4]{0,1:T(4,128)S(1)} %broadcast_multiply_fusion), channel_id=1, replica_groups=mesh['seq'=8,'tp'=4] {'tp'}, use_global_device_ids=true, to_apply=%region_8.9 | all-reduce | flops 2048 | bytes 16384 | tf_op jit(solution)/shard_map/psum | solution.py:141
  205.2 4.8 %convolution_bitcast_fusion = f32[1024,512]{0,1:T(8,128)} fusion(bf16[1024,1024]{1,0:T(8,128)(2,1)} %param.30, f32[512,1024]{1,0:T(8,128)} %get-tuple-element.77, f32[1024]{0:T(1024)S(1)} %copy-done.24, f32[512]{0:T(512)S(1)} %add_rsqrt_fusion), kind=kOutput, calls=%fused_computation.43 | convolution fusion | flops 1075314688 | bytes 6297600 | tf_op jit(solution)/shard_map/dot_general | solution.py:39
  210.1 47.7 %reduce-scatter.2.cloned.1.call-done = f32[256,512]{0,1:T(8,128)} async-done(((f32[1024,512]{0,1:T(8,128)}), f32[256,512]{0,1:T(8,128)}) %reduce-scatter.2.cloned.1.call-update) | async-done | bytes 524304 | tf_op jit(solution)/shard_map/reduce_scatter | solution.py:146
  257.7 1.8 convert_element_type.79
  259.5 29.3 %all-gather.5.cloned.1.call-done = bf16[1024,512]{0,1:T(8,128)(2,1)} async-done(((bf16[256,512]{0,1:T(8,128)(2,1)}), bf16[1024,512]{0,1:T(8,128)(2,1)}) %all-gather.5.cloned.1.call-update) | async-done | bytes 1048592 | tf_op jit(solution)/shard_map/all_gather | solution.py:149
  288.8 4.1 %fusion.21 = bf16[512,1024]{1,0:T(8,128)(2,1)} fusion(bf16[512,1024]{1,0:T(8,128)(2,1)S(1)} %copy-done.8, bf16[1024,512]{0,1:T(8,128)(2,1)} %all-gather.5.cloned.1.call-done, bf16[1024,1024]{1,0:T(8,128)(2,1)} %param.31), kind=kOutput, calls=%fused_computation.30 | convolution fusion | flops 1075314688 | bytes 5242880 | tf_op jit(solution)/shard_map/dot_general | solution.py:33
  (103 shorter events, 15.7 us)
Async XLA Ops:
  6.5 182.1 %copy-start = (bf16[1024,1024]{1,0:T(8,128)(2,1)S(1)}, bf16[1024,1024]{1,0:T(8,128)(2,1)}, u32[]{:S(2)}) copy-start(bf16[1024,1024]{1,0:T(8,128)(2,1)} %param.20) | copy-start | bytes 6291460
  6.5 93.8 %all-reduce.2.cloned.1.call-start = ((), (), s32[]{:S(2)}) async-start(), calls=%async_computation.1 | async-start | bytes 4194304 | tf_op jit(solution)/shard_map/psum | solution.py:79
  11.2 15.5 %copy-start.25 = (f32[16]{0:T(128)S(1)}, f32[16]{0:T(128)}, u32[]{:S(2)}) copy-start(f32[16]{0:T(128)} %param.27) | copy-start | bytes 196
  11.2 15.5 %copy-start.18 = (f32[4,256]{1,0:T(4,128)S(1)}, f32[4,256]{1,0:T(4,128)}, u32[]{:S(2)}) copy-start(f32[4,256]{1,0:T(4,128)} %param.25) | copy-start | bytes 12292
  11.2 16.2 %copy-start.17 = (f32[4,1024]{1,0:T(4,128)S(1)}, f32[4,1024]{1,0:T(4,128)}, u32[]{:S(2)}) copy-start(f32[4,1024]{1,0:T(4,128)} %param.24) | copy-start | bytes 49156
  11.2 169.1 %all-gather.7.cloned.1.call-start = ((), (), s32[]{:S(2)}) async-start(), calls=%async_computation.4 | async-start | bytes 4718592 | tf_op jit(solution)/shard_map/all_gather | solution.py:21
  12.7 89.4 %copy-start.23 = (bf16[1024,256]{1,0:T(8,128)(2,1)S(1)}, bf16[1024,256]{1,0:T(8,128)(2,1)}, u32[]{:S(2)}) copy-start(bf16[1024,256]{1,0:T(8,128)(2,1)} %param.22) | copy-start | bytes 1572868
  27.9 77.2 %copy-start.10 = (bf16[1024,16]{0,1:T(8,128)(2,1)S(1)}, bf16[1024,16]{0,1:T(8,128)(2,1)}, u32[]{:S(2)}) copy-start(bf16[1024,16]{0,1:T(8,128)(2,1)} %param.23) | copy-start | bytes 98308
  27.9 77.2 %copy-start.20 = (f32[16]{0:T(128)S(1)}, f32[16]{0:T(128)}, u32[]{:S(2)}) copy-start(f32[16]{0:T(128)} %param.26) | copy-start | bytes 196
  103.2 8.6 %collective-permute-start.1 = (bf16[3,256]{1,0:T(4,128)(2,1)}, bf16[3,256]{1,0:T(4,128)(2,1)}, u32[]{:S(2)}, u32[]{:S(2)}) collective-permute-start(bf16[3,256]{1,0:T(4,128)(2,1)} %slice.90), channel_id=1, source_target_pairs={{0,4},{4,8},{8,12},{12,16},{16,20},{20,24},{24,28},{1,5},{5,9},{9,... | collective-permute-start | bytes 4616 | tf_op jit(solution)/shard_map/ppermute | solution.py:16
  108.3 15.5 %collective-permute-start = (bf16[3,1024]{1,0:T(4,128)(2,1)S(1)}, bf16[3,1024]{1,0:T(4,128)(2,1)S(1)}, u32[]{:S(2)}, u32[]{:S(2)}) collective-permute-start(bf16[3,1024]{1,0:T(4,128)(2,1)S(1)} %slice.85), channel_id=1, source_target_pairs={{0,4},{4,8},{8,12},{12,16},{16,20},{20,24},{24,28},{1,5},{5,9},{9,... | collective-permute-start | bytes 18440 | tf_op jit(solution)/shard_map/ppermute | solution.py:16
  111.7 12.1 %copy-start.6 = (bf16[512,1024]{1,0:T(8,128)(2,1)S(1)}, bf16[512,1024]{1,0:T(8,128)(2,1)}, u32[]{:S(2)}) copy-start(bf16[512,1024]{1,0:T(8,128)(2,1)} %copy-done.5) | copy-start | bytes 3145732
  113.6 19.3 %copy-start.13 = (f32[1,1024]{1,0:T(1,128)S(1)}, f32[1,1024]{1,0:T(1,128)}, u32[]{:S(2)}) copy-start(f32[1,1024]{1,0:T(1,128)} %get-tuple-element.68) | copy-start | bytes 12292
  113.6 19.3 %copy-start.14 = (f32[1,1024]{1,0:T(1,128)S(1)}, f32[1,1024]{1,0:T(1,128)}, u32[]{:S(2)}) copy-start(f32[1,1024]{1,0:T(1,128)} %get-tuple-element.69) | copy-start | bytes 12292
  113.6 19.3 %copy-start.15 = (f32[1,1024]{1,0:T(1,128)S(1)}, f32[1,1024]{1,0:T(1,128)}, u32[]{:S(2)}) copy-start(f32[1,1024]{1,0:T(1,128)} %get-tuple-element.70) | copy-start | bytes 12292
  113.6 19.3 %copy-start.16 = (f32[1,1024]{1,0:T(1,128)S(1)}, f32[1,1024]{1,0:T(1,128)}, u32[]{:S(2)}) copy-start(f32[1,1024]{1,0:T(1,128)} %get-tuple-element.71) | copy-start | bytes 12292
  113.6 10.1 %collective-permute-start.2 = (bf16[512,256]{1,0:T(8,128)(2,1)S(1)}, bf16[512,256]{1,0:T(8,128)(2,1)S(1)}, u32[]{:S(2)}, u32[]{:S(2)}) collective-permute-start(bf16[512,256]{1,0:T(8,128)(2,1)S(1)} %multiply_convert_fusion.4), channel_id=1, source_target_pairs={{0,1},{1,2},{2,3},{3,0},{4,5},{5,6},{6,7},{7,4},{8,9},{9,10},{10,1... | collective-permute-start | bytes 786440 | tf_op jit(solution)/shard_map/ppermute | solution.py:95
  123.7 9.2 %collective-permute-start.3 = (bf16[512,256]{1,0:T(8,128)(2,1)S(1)}, bf16[512,256]{1,0:T(8,128)(2,1)S(1)}, u32[]{:S(2)}, u32[]{:S(2)}) collective-permute-start(bf16[512,256]{1,0:T(8,128)(2,1)S(1)} %collective-permute-done.2), channel_id=1, source_target_pairs={{0,1},{1,2},{2,3},{3,0},{4,5},{5,6},{6,7},{7,4},{8,9},{9,10},{10,1... | collective-permute-start | bytes 786440 | tf_op jit(solution)/shard_map/ppermute | solution.py:95
  132.9 8.3 %collective-permute-start.4 = (bf16[512,256]{1,0:T(8,128)(2,1)S(1)}, bf16[512,256]{1,0:T(8,128)(2,1)S(1)}, u32[]{:S(2)}, u32[]{:S(2)}) collective-permute-start(bf16[512,256]{1,0:T(8,128)(2,1)S(1)} %collective-permute-done.3), channel_id=1, source_target_pairs={{0,1},{1,2},{2,3},{3,0},{4,5},{5,6},{6,7},{7,4},{8,9},{9,10},{10,1... | collective-permute-start | bytes 786440 | tf_op jit(solution)/shard_map/ppermute | solution.py:95
  142.9 13.9 %copy-start.2 = (bf16[512,1024]{0,1:T(8,128)(2,1)S(1)}, bf16[512,1024]{0,1:T(8,128)(2,1)}, u32[]{:S(2)}) copy-start(bf16[512,1024]{0,1:T(8,128)(2,1)} %copy.29) | copy-start | bytes 3145732
  146.3 111.5 %reduce-scatter.2.cloned.1.call-start = ((), (), s32[]{:S(2)}) async-start(), calls=%async_computation.2 | async-start | bytes 2621440 | tf_op jit(solution)/shard_map/reduce_scatter | solution.py:146
  188.6 16.5 %copy-start.24 = (f32[1024]{0:T(1024)S(1)}, f32[1024]{0:T(1024)}, u32[]{:S(2)}) copy-start(f32[1024]{0:T(1024)} %param.29) | copy-start | bytes 12292
  210.0 78.8 %copy-start.8 = (bf16[512,1024]{1,0:T(8,128)(2,1)S(1)}, bf16[512,1024]{1,0:T(8,128)(2,1)}, u32[]{:S(2)}) copy-start(bf16[512,1024]{1,0:T(8,128)(2,1)} %param.17) | copy-start | bytes 3145732
  210.0 78.8 %all-gather.5.cloned.1.call-start = ((), (), s32[]{:S(2)}) async-start(), calls=%async_computation.3 | async-start | bytes 1310720 | tf_op jit(solution)/shard_map/all_gather | solution.py:149
  (11 other events, 27.5 us)
Sparse Core Ops, SparseCore 0:
  11.3 88.9 all-reduce.1
  146.4 33.8 all-gather.6
  210.1 47.5 reduce-scatter.1
  259.6 29.1 all-gather.4
